TPU v7x, 32 devices: a whole 2x2x4 slice. The times are simulated.
32 devices in a mesh: grp: 4 (over z), elem: 8 (over y, x, core).
Axes of the slice: x: 2, y: 2, z: 4, core: 2. Of those that a mesh axis runs over, the one named last changes fastest.
Arguments:
- velocity: float32 [3, 343, 4096], P(None, None, ('grp', 'elem')), may hold values from -0.6 to 0.6
- adjoint: float32 [3, 343, 4096], P(None, None, ('grp', 'elem')), may hold values from -0.6 to 0.6
- spacing: float32 [3, 4096], P(None, ('grp', 'elem')), may hold values from 0.5 to 2
- elem_count: int32 [32], P(('grp', 'elem')), may hold values from 32 to 128, as said below
- design_map: int32 [8, 4096], P(None, ('grp', 'elem')), may hold values from 0 to 65535, as said below
Outputs:
- direction: float32 [3, 65536], P(None, ('grp', 'elem'))
- objective: float32 [], replicated
Inputs may be any that keep to these rules, and one draw needn't show every extreme that they name: `elem_count`: the largest count equals 128 in every draw. `design_map`: design node d belongs to the device numbered d // 2048, counting grp first and elem second. Every entry of a device's columns names a node of a device whose elem index differs from that device's by at most one, cyclically over the elem axis, in any group.
All inputs are finite; a program needn't handle non-finite values.
Results may differ from a plain program's by a relative error of at most 0.0003.
Values sent between devices are 32-bit elements; how exact they have to be, the bound alone decides.
A program may use at most 64 MiB of HBM per device.

v0:
```python
import functools

import jax
import jax.numpy as jnp
import numpy as np
from jax import lax
from jax.experimental import pallas as pl
from jax.experimental.pallas import tpu as pltpu
from jax.sharding import PartitionSpec as P

P_SIZE = 7
ND_DEV = 2048
LANES = 128
UPPER = ND_DEV // LANES
NODES = P_SIZE**3
ROWS = -(-NODES // 16) * 16
HEAD = 240
BACK = 192
TAIL = ROWS - HEAD
MESH = pl.DeviceIdType.MESH
F32 = jnp.float32
BF16 = jnp.bfloat16


def lobatto(degree):
    points = np.cos(np.pi * np.arange(degree + 1) / degree)
    for sweep in range(60):
        lower = np.ones(degree + 1)
        upper = points.copy()
        for order in range(2, degree + 1):
            lower, upper = (upper, ((2 * order - 1) * points * upper - (order - 1) * lower) / order)
        points = points - (points * upper - lower) / ((degree + 1) * upper)
    lower = np.ones(degree + 1)
    upper = points.copy()
    for order in range(2, degree + 1):
        lower, upper = (upper, ((2 * order - 1) * points * upper - (order - 1) * lower) / order)
    return (points[::-1].copy(), upper[::-1].copy())


def halves(table):
    exact = np.asarray(table, np.float32)
    high = exact.astype(BF16)
    low = (exact - high.astype(np.float32)).astype(BF16)
    return (high, low)


def derivative_table():
    degree = P_SIZE - 1
    points, values = lobatto(degree)
    derivative = np.zeros((P_SIZE, P_SIZE))
    for i in range(P_SIZE):
        for j in range(P_SIZE):
            if i != j:
                derivative[i, j] = values[i] / (values[j] * (points[i] - points[j]))
    derivative[0, 0] = -degree * (degree + 1) / 4.0
    derivative[P_SIZE - 1, P_SIZE - 1] = degree * (degree + 1) / 4.0
    return derivative


def tables():
    degree = P_SIZE - 1
    points, values = lobatto(degree)
    weights = 2.0 / (degree * (degree + 1) * values**2)
    derivative = derivative_table()
    coords = np.meshgrid(points, points, points, indexing="ij")
    coords = [c.reshape(-1) for c in coords]
    spread = np.meshgrid(weights, weights, weights, indexing="ij")
    quadrature = (spread[0] * spread[1] * spread[2]).reshape(-1)
    contract = np.zeros((32, ROWS))
    for vertex in range(8):
        signs = [2.0 * (vertex >> 2 - m & 1) - 1.0 for m in range(3)]
        factors = [(1.0 + signs[m] * coords[m]) / 2.0 for m in range(3)]
        for j in range(3):
            others = [factors[m] for m in range(3) if m != j]
            contract[8 * j + vertex, :NODES] = signs[j] / 2.0 * others[0] * others[1] * quadrature
    contract[24, :NODES] = quadrature
    unit = np.eye(P_SIZE)
    near = np.zeros((2, ROWS, NODES))
    near[0, :NODES] = np.kron(np.kron(unit, derivative), unit)
    near[1, :NODES] = np.kron(np.kron(unit, unit), derivative)
    return (
        np.stack(halves(near[:, :HEAD, :256].reshape(2 * HEAD, 256))),
        np.stack(halves(near[:, HEAD:, BACK:].reshape(2 * TAIL, NODES - BACK))),
        np.concatenate(halves(contract)),
    )


def split(value):
    high = value.astype(BF16)
    return (high, (value - high.astype(F32)).astype(BF16))


def far_derivatives(velocity, adjoint, far):
    table = derivative_table()
    width = P_SIZE * P_SIZE
    for f, field in enumerate((velocity, adjoint)):
        for i in range(3):
            far[3 * f + i, ROWS - 16 :, :] = jnp.zeros((16, field.shape[2]), F32)
            slabs = [field[i, pl.ds(width * a, width), :] for a in range(P_SIZE)]
            for a in range(P_SIZE):
                far[3 * f + i, pl.ds(width * a, width), :] = sum(
                    float(table[a, b]) * slabs[b] for b in range(P_SIZE)
                )


def near_derivatives(fields, head, tail):
    high, low = split(fields)

    def apply(table, begin, end):
        return (
            jnp.dot(table[0], high[begin:end], preferred_element_type=F32)
            + jnp.dot(table[1], high[begin:end], preferred_element_type=F32)
            + jnp.dot(table[0], low[begin:end], preferred_element_type=F32)
        )

    upper = apply(head, 0, 256)
    lower = apply(tail, BACK, NODES)
    return [
        jnp.concatenate([upper[j * HEAD : (j + 1) * HEAD], lower[j * TAIL : (j + 1) * TAIL]], axis=0)
        for j in range(2)
    ]


def element_terms(far, near, spacing, live, contract):
    slots = spacing.shape[1]

    def grad(field, i, j):
        column = (3 * field + i) * slots
        return near[j - 1][:, column : column + slots] if j else far[3 * field + i]

    def product(c, j):
        return sum(grad(0, i, c) * grad(1, i, j) for i in range(3))

    pairs = [(0, 1), (0, 2), (1, 2)]
    stack = [product(m, m) for m in range(3)]
    stack += [product(c, j) + product(j, c) for c, j in pairs]
    stack += [sum(grad(0, i, j) * grad(0, i, j) for i in range(3)) for j in range(3)]
    stack_high, stack_low = split(jnp.concatenate(stack, axis=1))
    both = jnp.dot(contract, stack_high, preferred_element_type=F32)
    sums = both[:32] + both[32:] + jnp.dot(contract[:32], stack_low, preferred_element_type=F32)

    def part(j, column):
        return sums[8 * j : 8 * j + 8, column * slots : (column + 1) * slots]

    factor = [2.0 / spacing[j : j + 1] for j in range(3)]
    square = [f * f for f in factor]
    jacobian = spacing[0:1] * spacing[1:2] * spacing[2:3] * 0.125
    terms = []
    for c in range(3):
        total = sum(square[m] * part(c, m) for m in range(3)) - 2.0 * square[c] * part(c, c)
        for column, pair in enumerate(pairs):
            if c in pair:
                j = pair[0] + pair[1] - c
                total = total - square[j] * part(j, 3 + column)
        terms.append(jnp.where(live, total * (factor[c] * jacobian), 0.0))
    spent = sum(square[j] * part(3, 6 + j) for j in range(3)) * jacobian
    return (terms, jnp.where(live, spent, 0.0))


def place(index, rows, values=None):
    slots = index.shape[1]
    row = lax.broadcasted_iota(jnp.int32, (rows, slots), 0)
    columns = []
    for k in range(8):
        hit = row == index[k : k + 1]
        if values is None:
            columns.append(jnp.where(hit, 1.0, 0.0).astype(BF16))
        else:
            columns.append(
                jnp.concatenate(
                    [jnp.where(hit, v[k : k + 1], 0.0).astype(BF16) for v in values], axis=0
                )
            )
    return jnp.concatenate(columns, axis=1)


def kernel(
    groups, columns,
    velocity_in, adjoint_in, spacing_in, count_in, map_in, head_in, tail_in, contract_in,
    direction, objective,
    velocity, adjoint, spacing, count, design_map, head, tail, contract, far,
    outgoing, maps, arrived, placed, gathered,
    local_sem, send_map, recv_map, send_sem, recv_sem, send_all, recv_all,
):
    devices = groups * columns
    grp, col = lax.axis_index("grp"), lax.axis_index("elem")
    me = grp * columns + col
    slots = spacing.shape[1]

    barrier = pltpu.get_barrier_semaphore()
    pairs = [
        (velocity_in, velocity), (adjoint_in, adjoint), (head_in, head), (tail_in, tail),
        (map_in, design_map), (spacing_in, spacing), (count_in, count), (contract_in, contract),
    ]
    loads = [pltpu.make_async_copy(a, b, local_sem.at[i]) for i, (a, b) in enumerate(pairs)]
    for load in loads:
        load.start()

    def coords(step):
        peer = lax.rem(me + step, devices)
        return (peer // columns, lax.rem(peer, columns))

    def greet(step, carry):
        pl.semaphore_signal(barrier, inc=1, device_id=coords(step), device_id_type=MESH)
        return carry

    lax.fori_loop(1, devices, greet, 0)
    for load in loads[:4]:
        load.wait()

    fields = jnp.concatenate([f[i] for f in (velocity, adjoint) for i in range(3)], axis=1)
    near = near_derivatives(fields, head, tail)
    far_derivatives(velocity, adjoint, far)

    for load in loads[4:]:
        load.wait()
    pl.semaphore_wait(barrier, devices - 1)
    own = groups
    partners = []
    for step in [*range(groups // 2, groups), *range(groups // 2)]:
        for o in range(3):
            slot = o * groups + step
            if slot != own:
                there = (lax.rem(grp + step, groups), lax.rem(col + (o - 1 + columns), columns))
                partners.append((slot, there))

    def copies(source, target, send, receive):
        return {
            slot: pltpu.make_async_remote_copy(
                src_ref=source,
                dst_ref=target.at[slot],
                send_sem=send.at[slot],
                recv_sem=receive.at[slot],
                device_id=there,
                device_id_type=MESH,
            )
            for slot, there in partners
        }

    map_copies = copies(design_map, maps, send_map, recv_map)
    for copy in map_copies.values():
        copy.start()

    live = lax.broadcasted_iota(jnp.int32, (8, slots), 1) < count[0]
    terms, spent = element_terms(far, near, spacing[...], live, contract[...])
    for c in range(3):
        outgoing[8 * c : 8 * c + 8, :] = terms[c]
    term_copies = copies(outgoing, arrived, send_sem, recv_sem)
    for copy in term_copies.values():
        copy.start()

    base = me * UPPER

    def collect(nodes, term, lower):
        index = lax.shift_right_logical(nodes, jnp.full_like(nodes, LANES.bit_length() - 1)) - base
        highs = [term[8 * c : 8 * c + 8].astype(BF16).astype(F32) for c in range(3)]
        lows = [term[8 * c : 8 * c + 8] - highs[c] for c in range(3)]
        return lax.dot_general(
            place(index, UPPER, highs + lows),
            lower,
            (((1,), (1,)), ((), ())),
            preferred_element_type=F32,
        )

    nodes = design_map[...]
    both = collect(nodes, outgoing[...], place(nodes & (LANES - 1), LANES))
    for slot, copy in map_copies.items():
        copy.wait()
        placed[slot] = place(maps[slot] & (LANES - 1), LANES)

    for slot, copy in list(term_copies.items())[::-1]:
        copy.wait_recv()
        both = both + collect(maps[slot], arrived[slot], placed[slot])
    total = both[: 3 * UPPER] + both[3 * UPPER :]

    squares = total * total
    squares = sum(squares[8 * i : 8 * i + 8] for i in range(3 * UPPER // 8))
    lane = lax.broadcasted_iota(jnp.int32, (8, LANES), 1)
    mixed = jnp.where(
        lane < LANES // 2,
        squares + pltpu.roll(squares, LANES // 2, 1),
        spent + pltpu.roll(spent, LANES // 2, 1),
    )
    gathered[me] = jnp.sum(mixed, axis=0, keepdims=True)

    def share(step):
        return pltpu.make_async_remote_copy(
            src_ref=gathered.at[me],
            dst_ref=gathered.at[me],
            send_sem=send_all.at[step],
            recv_sem=recv_all.at[step],
            device_id=coords(step),
            device_id_type=MESH,
        )

    def send(step, carry):
        share(step).start()
        return carry

    def receive(step, carry):
        share(step).wait_recv()
        return carry

    def finish(step, carry):
        share(step).wait_send()
        return carry

    lax.fori_loop(1, devices, send, 0)
    for copy in term_copies.values():
        copy.wait_send()
    lax.fori_loop(1, devices, receive, 0)
    everything = jnp.sum(gathered[...], axis=0)
    first = lax.broadcasted_iota(jnp.int32, (1, LANES), 1) < LANES // 2
    square_total = jnp.sum(jnp.where(first, everything, 0.0), axis=1, keepdims=True)
    spent_total = jnp.sum(jnp.where(first, 0.0, everything), axis=1, keepdims=True)
    scale = lax.rsqrt(square_total * (1.0 / (3.0 * ND_DEV * devices)) + 1e-06)
    scaled = total * scale
    for c in range(3):
        direction[c] = scaled[UPPER * c : UPPER * c + UPPER]
    objective[...] = spent_total * (1.0 / (NODES * slots * devices))
    lax.fori_loop(1, devices, finish, 0)


def body(groups, columns, velocity, adjoint, spacing, elem_count, design_map):
    devices = groups * columns
    blocks = 3 * groups
    slots = spacing.shape[1]
    vmem = pl.BlockSpec(memory_space=pltpu.VMEM)
    constants = tables()
    direction, objective = pl.pallas_call(
        functools.partial(kernel, groups, columns),
        out_shape=(
            jax.ShapeDtypeStruct((3, UPPER, LANES), F32),
            jax.ShapeDtypeStruct((1, 1), F32),
        ),
        in_specs=[pl.BlockSpec(memory_space=pl.ANY)] * 8,
        out_specs=(vmem, vmem),
        scratch_shapes=[
            pltpu.VMEM(velocity.shape, F32),
            pltpu.VMEM(adjoint.shape, F32),
            pltpu.VMEM(spacing.shape, F32),
            pltpu.SMEM((1,), jnp.int32),
            pltpu.VMEM((8, slots), jnp.int32),
            *[pltpu.VMEM(table.shape, BF16) for table in constants],
            pltpu.VMEM((6, ROWS, slots), F32),
            pltpu.VMEM((24, slots), F32),
            pltpu.VMEM((blocks, 8, slots), jnp.int32),
            pltpu.VMEM((blocks, 24, slots), F32),
            pltpu.VMEM((blocks, LANES, 8 * slots), BF16),
            pltpu.VMEM((devices, 1, LANES), F32),
            pltpu.SemaphoreType.DMA((8,)),
            *[pltpu.SemaphoreType.DMA((blocks,))] * 4,
            *[pltpu.SemaphoreType.DMA((devices,))] * 2,
        ],
        compiler_params=pltpu.CompilerParams(collective_id=0, has_side_effects=True),
    )(velocity, adjoint, spacing, elem_count, design_map, *constants)
    return (direction.reshape(3, ND_DEV), objective.reshape(()))


def solution(mesh):
    return jax.shard_map(
        functools.partial(body, mesh.shape["grp"], mesh.shape["elem"]),
        mesh=mesh,
        in_specs=(
            P(None, None, ("grp", "elem")),
            P(None, None, ("grp", "elem")),
            P(None, ("grp", "elem")),
            P(("grp", "elem")),
            P(None, ("grp", "elem")),
        ),
        out_specs=(P(None, ("grp", "elem")), P()),
        check_vma=False,
    )
```

profile of v0, /device:TPU:0, one launch (start us, length us, event | category | flops | bytes accessed | tf_op | source)
XLA Modules:
  0.0 25.6 jit_solution(2626034407970317586)
XLA Ops:
  1.3 21.2 %shard_map.95 = (f32[3,16,128]{2,1,0:T(8,128)}, f32[1,1]{1,0:T(1,128)}) custom-call(f32[3,343,128]{2,1,0:T(8,128)} %velocity_in.1, f32[3,343,128]{2,1,0:T(8,128)} %adjoint_in.1, f32[3,128]{1,0:T(4,128)} %spacing_in.1, s32[1]{0:T(128)S(6)} %copy.14.count_in, s32[8,128]{1,0:T(8,128)} %map_in.1, bf16[2,480,256]{2,1,0:T(8,128)(2,1)} %constant.6.clone.head_in, ...), custom_call_target="tpu_custom_call" | custom-call | tf_op jit(solution)/shard_map/pallas_call | solution.py:330
  22.5 1.4 %copy.12 = f32[1,3,16,128]{3,1,2,0:T(4,128)} copy(f32[1,3,16,128]{3,2,1,0:T(8,128)} %bitcast.6) | data formatting | bytes 49152
where the time goes:
time: 25.8 us; the launch traced here: 25.6 us
  Pallas kernels  21.2 us (82%)
  between operations  3.05 us (12%)
  local copies, waits for them, and re-layouts  1.37 us (5%)
    pallas_call x1, Pallas kernels, body(): pl.pallas_call(functools.partial(kernel, groups, columns), out_shape=(jax...  21.2 us
    unnamed x1, local copies, waits for them, and re-layouts  1.37 us

commit v1 on v0

--- a/solution.py
+++ b/solution.py
@@ -20,6 +20,7 @@
 MESH = pl.DeviceIdType.MESH
 F32 = jnp.float32
 BF16 = jnp.bfloat16
+VMEM_BYTES = 32 * 2**20
 
 
 def lobatto(degree):
@@ -174,6 +175,19 @@
     return jnp.concatenate(columns, axis=1)
 
 
+def far_first(groups, grp):
+    place = jnp.minimum(grp, groups - 1 - grp)
+    sign = 1 - 2 * (2 * grp // groups)
+    single = groups - 1 - 2 * place
+    steps = []
+    for turn in range(groups - 1):
+        rest = turn - single
+        pair = (place - rest // 2) * (1 - 2 * lax.rem(rest + 2 * groups, 2))
+        offset = jnp.where(rest < 0, groups - 1 - place - turn, pair)
+        steps.append(lax.rem(sign * offset + groups, groups))
+    return steps
+
+
 def kernel(
     groups, columns,
     velocity_in, adjoint_in, spacing_in, count_in, map_in, head_in, tail_in, contract_in,
@@ -196,15 +210,15 @@
     for load in loads:
         load.start()
 
-    def coords(step):
-        peer = lax.rem(me + step, devices)
-        return (peer // columns, lax.rem(peer, columns))
-
-    def greet(step, carry):
-        pl.semaphore_signal(barrier, inc=1, device_id=coords(step), device_id_type=MESH)
-        return carry
-
-    lax.fori_loop(1, devices, greet, 0)
+    steps = far_first(groups, grp)
+
+    def at(step, turn):
+        return (lax.rem(grp + step, groups), lax.rem(col + turn, columns))
+
+    everyone = [(step, turn) for step in steps for turn in range(columns)]
+    everyone += [(0, turn) for turn in range(1, columns)]
+    for step, turn in everyone:
+        pl.semaphore_signal(barrier, inc=1, device_id=at(step, turn), device_id_type=MESH)
     for load in loads[:4]:
         load.wait()
 
@@ -214,40 +228,35 @@
 
     for load in loads[4:]:
         load.wait()
-    pl.semaphore_wait(barrier, devices - 1)
-    own = groups
-    partners = []
-    for step in [*range(groups // 2, groups), *range(groups // 2)]:
-        for o in range(3):
-            slot = o * groups + step
-            if slot != own:
-                there = (lax.rem(grp + step, groups), lax.rem(col + (o - 1 + columns), columns))
-                partners.append((slot, there))
-
-    def copies(source, target, send, receive):
-        return {
-            slot: pltpu.make_async_remote_copy(
-                src_ref=source,
-                dst_ref=target.at[slot],
-                send_sem=send.at[slot],
-                recv_sem=receive.at[slot],
-                device_id=there,
-                device_id_type=MESH,
-            )
-            for slot, there in partners
-        }
-
-    map_copies = copies(design_map, maps, send_map, recv_map)
-    for copy in map_copies.values():
-        copy.start()
+    def copy(source, target, send, receive, o, step):
+        slot = o * groups + step
+        return pltpu.make_async_remote_copy(
+            src_ref=source,
+            dst_ref=target.at[slot],
+            send_sem=send.at[slot],
+            recv_sem=receive.at[slot],
+            device_id=at(step, (o + columns - 1) % columns),
+            device_id_type=MESH,
+        )
+
+    sends = [(o, step) for step in steps for o in (0, 2, 1)] + [(0, 0), (2, 0)]
+    waits = [(o, step) for step in range(groups) for o in (1, 0, 2) if o != 1 or step]
+
+    def map_copy(o, step):
+        return copy(design_map, maps, send_map, recv_map, o, step)
+
+    def term_copy(o, step):
+        return copy(outgoing, arrived, send_sem, recv_sem, o, step)
 
     live = lax.broadcasted_iota(jnp.int32, (8, slots), 1) < count[0]
     terms, spent = element_terms(far, near, spacing[...], live, contract[...])
     for c in range(3):
         outgoing[8 * c : 8 * c + 8, :] = terms[c]
-    term_copies = copies(outgoing, arrived, send_sem, recv_sem)
-    for copy in term_copies.values():
-        copy.start()
+    pl.semaphore_wait(barrier, devices - 1)
+    for o, step in sends:
+        map_copy(o, step).start()
+    for o, step in sends:
+        term_copy(o, step).start()
 
     base = me * UPPER
 
@@ -264,12 +273,14 @@
 
     nodes = design_map[...]
     both = collect(nodes, outgoing[...], place(nodes & (LANES - 1), LANES))
-    for slot, copy in map_copies.items():
-        copy.wait()
+    for o, step in waits:
+        slot = o * groups + step
+        map_copy(o, step).wait()
         placed[slot] = place(maps[slot] & (LANES - 1), LANES)
 
-    for slot, copy in list(term_copies.items())[::-1]:
-        copy.wait_recv()
+    for o, step in waits:
+        slot = o * groups + step
+        term_copy(o, step).wait_recv()
         both = both + collect(maps[slot], arrived[slot], placed[slot])
     total = both[: 3 * UPPER] + both[3 * UPPER :]
 
@@ -281,34 +292,25 @@
         squares + pltpu.roll(squares, LANES // 2, 1),
         spent + pltpu.roll(spent, LANES // 2, 1),
     )
-    gathered[me] = jnp.sum(mixed, axis=0, keepdims=True)
-
-    def share(step):
+    gathered[devices - 1] = jnp.sum(mixed, axis=0, keepdims=True)
+
+    def share(step, turn):
+        slot = step * columns + turn - 1
         return pltpu.make_async_remote_copy(
-            src_ref=gathered.at[me],
-            dst_ref=gathered.at[me],
-            send_sem=send_all.at[step],
-            recv_sem=recv_all.at[step],
-            device_id=coords(step),
+            src_ref=gathered.at[devices - 1],
+            dst_ref=gathered.at[slot],
+            send_sem=send_all.at[slot],
+            recv_sem=recv_all.at[slot],
+            device_id=at(step, turn),
             device_id_type=MESH,
         )
 
-    def send(step, carry):
-        share(step).start()
-        return carry
-
-    def receive(step, carry):
-        share(step).wait_recv()
-        return carry
-
-    def finish(step, carry):
-        share(step).wait_send()
-        return carry
-
-    lax.fori_loop(1, devices, send, 0)
-    for copy in term_copies.values():
-        copy.wait_send()
-    lax.fori_loop(1, devices, receive, 0)
+    for step, turn in everyone:
+        share(step, turn).start()
+    for o, step in sends:
+        term_copy(o, step).wait_send()
+    for step, turn in everyone:
+        share(step, turn).wait_recv()
     everything = jnp.sum(gathered[...], axis=0)
     first = lax.broadcasted_iota(jnp.int32, (1, LANES), 1) < LANES // 2
     square_total = jnp.sum(jnp.where(first, everything, 0.0), axis=1, keepdims=True)
@@ -317,8 +319,16 @@
     scaled = total * scale
     for c in range(3):
         direction[c] = scaled[UPPER * c : UPPER * c + UPPER]
-    objective[...] = spent_total * (1.0 / (NODES * slots * devices))
-    lax.fori_loop(1, devices, finish, 0)
+    objective[...] = jnp.broadcast_to(spent_total * (1.0 / (NODES * slots * devices)), (1, LANES))
+    for step, turn in everyone:
+        share(step, turn).wait_send()
+
+
+def hand_over(scaled, spent, direction, objective):
+    for c in range(3):
+        for u in range(UPPER):
+            direction[c : c + 1, u * LANES : (u + 1) * LANES] = scaled[c, u : u + 1, :]
+    objective[...] = spent[:, :1]
 
 
 def body(groups, columns, velocity, adjoint, spacing, elem_count, design_map):
@@ -327,13 +337,22 @@
     slots = spacing.shape[1]
     vmem = pl.BlockSpec(memory_space=pltpu.VMEM)
     constants = tables()
-    direction, objective = pl.pallas_call(
+    operands = [
+        pltpu.with_memory_space_constraint(jnp.asarray(x), pltpu.HBM)
+        for x in (velocity, adjoint, spacing)
+    ]
+    operands.append(elem_count)
+    operands += [
+        pltpu.with_memory_space_constraint(jnp.asarray(x), pltpu.HBM)
+        for x in (design_map, *constants)
+    ]
+    scaled, spent = pl.pallas_call(
         functools.partial(kernel, groups, columns),
         out_shape=(
             jax.ShapeDtypeStruct((3, UPPER, LANES), F32),
-            jax.ShapeDtypeStruct((1, 1), F32),
+            jax.ShapeDtypeStruct((1, LANES), F32),
         ),
-        in_specs=[pl.BlockSpec(memory_space=pl.ANY)] * 8,
+        in_specs=[pl.BlockSpec(memory_space=pltpu.HBM)] * 8,
         out_specs=(vmem, vmem),
         scratch_shapes=[
             pltpu.VMEM(velocity.shape, F32),
@@ -352,9 +371,21 @@
             *[pltpu.SemaphoreType.DMA((blocks,))] * 4,
             *[pltpu.SemaphoreType.DMA((devices,))] * 2,
         ],
-        compiler_params=pltpu.CompilerParams(collective_id=0, has_side_effects=True),
-    )(velocity, adjoint, spacing, elem_count, design_map, *constants)
-    return (direction.reshape(3, ND_DEV), objective.reshape(()))
+        compiler_params=pltpu.CompilerParams(
+            collective_id=0, has_side_effects=True, vmem_limit_bytes=VMEM_BYTES
+        ),
+    )(*operands)
+    direction, objective = pl.pallas_call(
+        hand_over,
+        out_shape=(
+            jax.ShapeDtypeStruct((3, ND_DEV), F32),
+            jax.ShapeDtypeStruct((1, 1), F32),
+        ),
+        in_specs=[vmem] * 2,
+        out_specs=(vmem, vmem),
+        compiler_params=pltpu.CompilerParams(vmem_limit_bytes=VMEM_BYTES),
+    )(scaled, spent)
+    return (direction, objective.reshape(()))
 
 
 def solution(mesh):

time: 25.8 us -> 22 us (0.85)
  between operations: 3.05 us -> 1.28 us
  local copies, waits for them, and re-layouts: 1.37 us -> 0 us
  Pallas kernels: 21.2 us -> 20.5 us
    unnamed x1 -> x0, local copies, waits for them, and re-layouts: 1.37 us -> none
    pallas_call x1, Pallas kernels: 21.2 us -> 19.9 us  [body(): pl.pallas_call(functools.partial(kernel, groups, columns), out_shape=(jax...]
    pallas_call x0 -> x1, Pallas kernels: none -> 0.64 us  [body(): pl.pallas_call(hand_over, out_shape=(jax.ShapeDtypeStruct((3, ND_DEV), F3...]
where the time goes in v1:
time: 22 us; the launch traced here: 21.8 us
  Pallas kernels  20.5 us (93%)
  between operations  1.28 us (6%)
    pallas_call x1, Pallas kernels, body(): pl.pallas_call(functools.partial(kernel, groups, columns), out_shape=(jax...  19.9 us
    pallas_call x1, Pallas kernels, body(): pl.pallas_call(hand_over, out_shape=(jax.ShapeDtypeStruct((3, ND_DEV), F3...  0.64 us

profile of v1, /device:TPU:0, one launch (start us, length us, event | category | flops | bytes accessed | tf_op | source)
XLA Modules:
  0.0 21.8 jit_solution(18058355790502660666)
XLA Ops:
  1.3 19.9 %shard_map.95 = (f32[3,16,128]{2,1,0:T(8,128)S(1)}, f32[1,128]{1,0:T(1,128)S(1)}) custom-call(f32[3,343,128]{2,1,0:T(8,128)} %velocity_in.1, f32[3,343,128]{2,1,0:T(8,128)} %adjoint_in.1, f32[3,128]{1,0:T(4,128)} %spacing_in.1, s32[1]{0:T(128)S(6)} %copy.10.count_in, s32[8,128]{1,0:T(8,128)} %map_in.1, bf16[2,480,256]{2,1,0:T(8,128)(2,1)} %constant.6.clone.head_in, ...), custom_call_target="tpu_custom_call" | custom-call | tf_op jit(solution)/shard_map/pallas_call | solution.py:349
  21.2 0.6 %shard_map.96 = (f32[3,2048]{1,0:T(4,128)}, f32[1,1]{1,0:T(1,128)}) custom-call(f32[3,16,128]{2,1,0:T(8,128)S(1)} %get-tuple-element.6.scaled, f32[1,128]{1,0:T(1,128)S(1)} %get-tuple-element.7.spent), custom_call_target="tpu_custom_call" | custom-call | tf_op jit(solution)/shard_map/pallas_call | solution.py:378

commit v2 on v1

--- a/solution.py
+++ b/solution.py
@@ -193,8 +193,8 @@
     velocity_in, adjoint_in, spacing_in, count_in, map_in, head_in, tail_in, contract_in,
     direction, objective,
     velocity, adjoint, spacing, count, design_map, head, tail, contract, far,
-    outgoing, maps, arrived, placed, gathered,
-    local_sem, send_map, recv_map, send_sem, recv_sem, send_all, recv_all,
+    outgoing, arrived, gathered,
+    local_sem, send_sem, recv_sem, hand_sem, send_all, recv_all,
 ):
     devices = groups * columns
     grp, col = lax.axis_index("grp"), lax.axis_index("elem")
@@ -228,39 +228,67 @@
 
     for load in loads[4:]:
         load.wait()
-    def copy(source, target, send, receive, o, step):
-        slot = o * groups + step
+    odd = lax.rem(col, 2)
+    partner = col + 1 - 2 * odd
+    outer = lax.rem(col + 2 * odd + columns - 1, columns)
+
+    def message(slot, there):
         return pltpu.make_async_remote_copy(
-            src_ref=source,
-            dst_ref=target.at[slot],
-            send_sem=send.at[slot],
-            recv_sem=receive.at[slot],
-            device_id=at(step, (o + columns - 1) % columns),
+            src_ref=outgoing,
+            dst_ref=arrived.at[slot],
+            send_sem=send_sem,
+            recv_sem=recv_sem.at[slot],
+            device_id=there,
             device_id_type=MESH,
         )
 
-    sends = [(o, step) for step in steps for o in (0, 2, 1)] + [(0, 0), (2, 0)]
-    waits = [(o, step) for step in range(groups) for o in (1, 0, 2) if o != 1 or step]
-
-    def map_copy(o, step):
-        return copy(design_map, maps, send_map, recv_map, o, step)
-
-    def term_copy(o, step):
-        return copy(outgoing, arrived, send_sem, recv_sem, o, step)
+    def hand_on(slot):
+        return pltpu.make_async_remote_copy(
+            src_ref=arrived.at[slot],
+            dst_ref=arrived.at[slot],
+            send_sem=hand_sem,
+            recv_sem=recv_sem.at[slot],
+            device_id=(grp, partner),
+            device_id_type=MESH,
+        )
+
+    def whole(ref, count, semaphore):
+        part = ref.at[pl.ds(0, count)]
+        return pltpu.make_async_remote_copy(
+            src_ref=part,
+            dst_ref=part,
+            send_sem=semaphore,
+            recv_sem=semaphore,
+            device_id=(grp, partner),
+            device_id_type=MESH,
+        )
+
+    def along(parity, step):
+        return groups + parity * (groups - 1) + step
+
+    messages = []
+    for step in steps:
+        there = lax.rem(grp + step, groups)
+        messages.append(message(along(odd, step), (there, col + 1 - odd)))
+        messages.append(message(1 + step, (there, outer)))
+    messages.append(message(1, (grp, outer)))
+    messages.append(message(0, (grp, partner)))
 
     live = lax.broadcasted_iota(jnp.int32, (8, slots), 1) < count[0]
     terms, spent = element_terms(far, near, spacing[...], live, contract[...])
     for c in range(3):
         outgoing[8 * c : 8 * c + 8, :] = terms[c]
+    outgoing[24:32, :] = design_map[...].astype(F32)
     pl.semaphore_wait(barrier, devices - 1)
-    for o, step in sends:
-        map_copy(o, step).start()
-    for o, step in sends:
-        term_copy(o, step).start()
+    for copy in messages:
+        copy.start()
 
     base = me * UPPER
 
-    def collect(nodes, term, lower):
+    def collect(block):
+        nodes = block[24:32].astype(jnp.int32)
+        term = block[:24]
+        lower = place(nodes & (LANES - 1), LANES)
         index = lax.shift_right_logical(nodes, jnp.full_like(nodes, LANES.bit_length() - 1)) - base
         highs = [term[8 * c : 8 * c + 8].astype(BF16).astype(F32) for c in range(3)]
         lows = [term[8 * c : 8 * c + 8] - highs[c] for c in range(3)]
@@ -271,17 +299,19 @@
             preferred_element_type=F32,
         )
 
-    nodes = design_map[...]
-    both = collect(nodes, outgoing[...], place(nodes & (LANES - 1), LANES))
-    for o, step in waits:
-        slot = o * groups + step
-        map_copy(o, step).wait()
-        placed[slot] = place(maps[slot] & (LANES - 1), LANES)
-
-    for o, step in waits:
-        slot = o * groups + step
-        term_copy(o, step).wait_recv()
-        both = both + collect(maps[slot], arrived[slot], placed[slot])
+    both = collect(outgoing[...])
+    order = [(0, False), (1, False)]
+    for step in steps[::-1]:
+        order += [(along(0, step), True), (along(1, step), True), (1 + step, False)]
+    for slot, shared in order:
+        hand_on(slot).wait_recv()
+        if shared:
+
+            @pl.when(odd == 1)
+            def _():
+                hand_on(slot).start()
+
+        both = both + collect(arrived[slot])
     total = both[: 3 * UPPER] + both[3 * UPPER :]
 
     squares = total * total
@@ -299,18 +329,16 @@
         return pltpu.make_async_remote_copy(
             src_ref=gathered.at[devices - 1],
             dst_ref=gathered.at[slot],
-            send_sem=send_all.at[slot],
-            recv_sem=recv_all.at[slot],
+            send_sem=send_all,
+            recv_sem=recv_all,
             device_id=at(step, turn),
             device_id_type=MESH,
         )
 
     for step, turn in everyone:
         share(step, turn).start()
-    for o, step in sends:
-        term_copy(o, step).wait_send()
-    for step, turn in everyone:
-        share(step, turn).wait_recv()
+    whole(arrived, len(messages), send_sem).wait_send()
+    whole(gathered, devices - 1, recv_all).wait_recv()
     everything = jnp.sum(gathered[...], axis=0)
     first = lax.broadcasted_iota(jnp.int32, (1, LANES), 1) < LANES // 2
     square_total = jnp.sum(jnp.where(first, everything, 0.0), axis=1, keepdims=True)
@@ -320,8 +348,11 @@
     for c in range(3):
         direction[c] = scaled[UPPER * c : UPPER * c + UPPER]
     objective[...] = jnp.broadcast_to(spent_total * (1.0 / (NODES * slots * devices)), (1, LANES))
-    for step, turn in everyone:
-        share(step, turn).wait_send()
+    whole(gathered, devices - 1, send_all).wait_send()
+
+    @pl.when(odd == 1)
+    def _():
+        whole(arrived, 2 * (groups - 1), hand_sem).wait_send()
 
 
 def hand_over(scaled, spent, direction, objective):
@@ -362,14 +393,13 @@
             pltpu.VMEM((8, slots), jnp.int32),
             *[pltpu.VMEM(table.shape, BF16) for table in constants],
             pltpu.VMEM((6, ROWS, slots), F32),
-            pltpu.VMEM((24, slots), F32),
-            pltpu.VMEM((blocks, 8, slots), jnp.int32),
-            pltpu.VMEM((blocks, 24, slots), F32),
-            pltpu.VMEM((blocks, LANES, 8 * slots), BF16),
+            pltpu.VMEM((32, slots), F32),
+            pltpu.VMEM((blocks - 1, 32, slots), F32),
             pltpu.VMEM((devices, 1, LANES), F32),
             pltpu.SemaphoreType.DMA((8,)),
-            *[pltpu.SemaphoreType.DMA((blocks,))] * 4,
-            *[pltpu.SemaphoreType.DMA((devices,))] * 2,
+            pltpu.SemaphoreType.DMA,
+            pltpu.SemaphoreType.DMA((blocks - 1,)),
+            *[pltpu.SemaphoreType.DMA] * 3,
         ],
         compiler_params=pltpu.CompilerParams(
             collective_id=0, has_side_effects=True, vmem_limit_bytes=VMEM_BYTES

time: 22 us -> 20.7 us (0.941)
  Pallas kernels: 20.5 us -> 19.3 us
    pallas_call x1, Pallas kernels: 19.9 us -> 18.7 us  [body(): pl.pallas_call(functools.partial(kernel, groups, columns), out_shape=(jax...]
where the time goes in v2:
time: 20.7 us; the launch traced here: 20.6 us
  Pallas kernels  19.3 us (93%)
  between operations  1.28 us (6%)
    pallas_call x1, Pallas kernels, body(): pl.pallas_call(functools.partial(kernel, groups, columns), out_shape=(jax...  18.7 us
    pallas_call x1, Pallas kernels, body(): pl.pallas_call(hand_over, out_shape=(jax.ShapeDtypeStruct((3, ND_DEV), F3...  0.64 us

profile of v2, /device:TPU:0, one launch (start us, length us, event | category | flops | bytes accessed | tf_op | source)
XLA Modules:
  0.0 20.6 jit_solution(6143725790655058707)
XLA Ops:
  1.3 18.7 %shard_map.95 = (f32[3,16,128]{2,1,0:T(8,128)S(1)}, f32[1,128]{1,0:T(1,128)S(1)}) custom-call(f32[3,343,128]{2,1,0:T(8,128)} %velocity_in.1, f32[3,343,128]{2,1,0:T(8,128)} %adjoint_in.1, f32[3,128]{1,0:T(4,128)} %spacing_in.1, s32[1]{0:T(128)S(6)} %copy.10.count_in, s32[8,128]{1,0:T(8,128)} %map_in.1, bf16[2,480,256]{2,1,0:T(8,128)(2,1)} %constant.6.clone.head_in, ...), custom_call_target="tpu_custom_call" | custom-call | tf_op jit(solution)/shard_map/pallas_call | solution.py:380
  19.9 0.6 %shard_map.96 = (f32[3,2048]{1,0:T(4,128)}, f32[1,1]{1,0:T(1,128)}) custom-call(f32[3,16,128]{2,1,0:T(8,128)S(1)} %get-tuple-element.6.scaled, f32[1,128]{1,0:T(1,128)S(1)} %get-tuple-element.7.spent), custom_call_target="tpu_custom_call" | custom-call | tf_op jit(solution)/shard_map/pallas_call | solution.py:408

commit v3 on v2

--- a/solution.py
+++ b/solution.py
@@ -13,10 +13,11 @@
 LANES = 128
 UPPER = ND_DEV // LANES
 NODES = P_SIZE**3
-ROWS = -(-NODES // 16) * 16
-HEAD = 240
-BACK = 192
-TAIL = ROWS - HEAD
+FACE = P_SIZE * P_SIZE
+CHUNKS = -(-FACE // 8)
+SLAB = 8 * CHUNKS
+DEEP = 64
+HALF = P_SIZE // 2
 MESH = pl.DeviceIdType.MESH
 F32 = jnp.float32
 BF16 = jnp.bfloat16
@@ -58,31 +59,42 @@
     return derivative
 
 
-def tables():
+def triple(table, rows):
+    wide = np.zeros((rows, DEEP))
+    wide[: table.shape[0], :FACE] = table
+    high, low = halves(wide)
+    return np.concatenate([high, high, low], axis=1)
+
+
+def quadrature():
     degree = P_SIZE - 1
     points, values = lobatto(degree)
-    weights = 2.0 / (degree * (degree + 1) * values**2)
+    return (points, 2.0 / (degree * (degree + 1) * values**2))
+
+
+def tables():
+    points, weights = quadrature()
     derivative = derivative_table()
-    coords = np.meshgrid(points, points, points, indexing="ij")
-    coords = [c.reshape(-1) for c in coords]
-    spread = np.meshgrid(weights, weights, weights, indexing="ij")
-    quadrature = (spread[0] * spread[1] * spread[2]).reshape(-1)
-    contract = np.zeros((32, ROWS))
+    unit = np.eye(P_SIZE)
+    near = [triple(t, SLAB) for t in (np.kron(derivative, unit), np.kron(unit, derivative))]
+    coords = [c.reshape(-1) for c in np.meshgrid(points, points, indexing="ij")]
+    face = np.outer(weights, weights).reshape(-1)
+    even = np.zeros((24, FACE))
+    uneven = np.zeros((24, FACE))
     for vertex in range(8):
         signs = [2.0 * (vertex >> 2 - m & 1) - 1.0 for m in range(3)]
-        factors = [(1.0 + signs[m] * coords[m]) / 2.0 for m in range(3)]
-        for j in range(3):
-            others = [factors[m] for m in range(3) if m != j]
-            contract[8 * j + vertex, :NODES] = signs[j] / 2.0 * others[0] * others[1] * quadrature
-    contract[24, :NODES] = quadrature
-    unit = np.eye(P_SIZE)
-    near = np.zeros((2, ROWS, NODES))
-    near[0, :NODES] = np.kron(np.kron(unit, derivative), unit)
-    near[1, :NODES] = np.kron(np.kron(unit, unit), derivative)
+        first, second = [(1.0 + signs[m + 1] * coords[m]) / 2.0 for m in range(2)]
+        even[vertex] = signs[0] / 2.0 * first * second * face
+        even[8 + vertex] = signs[1] / 4.0 * second * face
+        even[16 + vertex] = signs[2] / 4.0 * first * face
+        uneven[8 + vertex] = signs[0] * even[8 + vertex]
+        uneven[16 + vertex] = signs[0] * even[16 + vertex]
+    weigh = np.zeros((SLAB, LANES), np.float32)
+    weigh[:FACE] = face[:, None]
     return (
-        np.stack(halves(near[:, :HEAD, :256].reshape(2 * HEAD, 256))),
-        np.stack(halves(near[:, HEAD:, BACK:].reshape(2 * TAIL, NODES - BACK))),
-        np.concatenate(halves(contract)),
+        np.concatenate(near, axis=0),
+        np.concatenate([triple(even, 32), triple(uneven, 32)], axis=1),
+        weigh,
     )
 
 
@@ -91,86 +103,146 @@
     return (high, (value - high.astype(F32)).astype(BF16))
 
 
+def chunk(field, i, a, r):
+    start = FACE * a + 8 * r
+    if start + 8 <= NODES:
+        return field[i, pl.ds(start, 8), :]
+    rest = NODES - start
+    row = lax.broadcasted_iota(jnp.int32, (8, field.shape[2]), 0)
+    value = jnp.zeros((8, field.shape[2]), F32)
+    for k in range(rest):
+        value = jnp.where(row == k, field[i, pl.ds(start + k, 1), :], value)
+    return value
+
+
+def stacked(parts):
+    high, low = split(jnp.concatenate(parts, axis=0))
+    return jnp.concatenate([high, low, high], axis=0)
+
+
+def near_derivatives(velocity, adjoint, table, near):
+    blank = jnp.zeros((DEEP - SLAB, velocity.shape[2]), F32)
+    for a in range(P_SIZE):
+        fields = [
+            stacked([*[chunk(field, i, a, r) for r in range(CHUNKS)], blank])
+            for field in (velocity, adjoint)
+            for i in range(3)
+        ]
+        near[a] = jnp.dot(
+            table[...], jnp.concatenate(fields, axis=1), preferred_element_type=F32
+        )
+
+
 def far_derivatives(velocity, adjoint, far):
     table = derivative_table()
-    width = P_SIZE * P_SIZE
-    for f, field in enumerate((velocity, adjoint)):
-        for i in range(3):
-            far[3 * f + i, ROWS - 16 :, :] = jnp.zeros((16, field.shape[2]), F32)
-            slabs = [field[i, pl.ds(width * a, width), :] for a in range(P_SIZE)]
-            for a in range(P_SIZE):
-                far[3 * f + i, pl.ds(width * a, width), :] = sum(
-                    float(table[a, b]) * slabs[b] for b in range(P_SIZE)
+    for f in range(6):
+        field = (velocity, adjoint)[f // 3]
+        for r in range(CHUNKS):
+            x = [chunk(field, f % 3, a, r) for a in range(P_SIZE)]
+            plus = [x[j] + x[P_SIZE - 1 - j] for j in range(HALF)]
+            minus = [x[j] - x[P_SIZE - 1 - j] for j in range(HALF)]
+
+            def put(a, value):
+                far[f, a, 8 * r : 8 * r + 8, :] = value
+
+            for i in range(HALF):
+                mirror = table[i, ::-1]
+                even = float(table[i, HALF]) * x[HALF] + sum(
+                    float(table[i, j] + mirror[j]) / 2.0 * plus[j] for j in range(HALF)
                 )
-
-
-def near_derivatives(fields, head, tail):
-    high, low = split(fields)
-
-    def apply(table, begin, end):
-        return (
-            jnp.dot(table[0], high[begin:end], preferred_element_type=F32)
-            + jnp.dot(table[1], high[begin:end], preferred_element_type=F32)
-            + jnp.dot(table[0], low[begin:end], preferred_element_type=F32)
-        )
-
-    upper = apply(head, 0, 256)
-    lower = apply(tail, BACK, NODES)
-    return [
-        jnp.concatenate([upper[j * HEAD : (j + 1) * HEAD], lower[j * TAIL : (j + 1) * TAIL]], axis=0)
-        for j in range(2)
-    ]
-
-
-def element_terms(far, near, spacing, live, contract):
+                uneven = sum(float(table[i, j] - mirror[j]) / 2.0 * minus[j] for j in range(HALF))
+                put(i, uneven + even)
+                put(P_SIZE - 1 - i, uneven - even)
+            put(HALF, sum(float(table[HALF, j]) * minus[j] for j in range(HALF)))
+
+
+PAIRS = [(0, 1), (0, 2), (1, 2)]
+
+
+def reduced(far, near, r, slots):
+    points, weights = quadrature()
+
+    def products(a):
+        def grad(f, j):
+            if j == 0:
+                return far[f, a, 8 * r : 8 * r + 8, :]
+            row = SLAB * (j - 1) + 8 * r
+            return near[a, row : row + 8, f * slots : (f + 1) * slots]
+
+        u = [[grad(i, j) for j in range(3)] for i in range(3)]
+        w = [[grad(3 + i, j) for j in range(3)] for i in range(3)]
+        stress = [sum(u[i][m] * w[i][m] for i in range(3)) for m in range(3)]
+        stress += [
+            sum(u[i][c] * w[i][j] for i in range(3)) + sum(w[i][c] * u[i][j] for i in range(3))
+            for c, j in PAIRS
+        ]
+        return (stress, [sum(u[i][j] * u[i][j] for i in range(3)) for j in range(3)])
+
+    stress, spent = products(HALF)
+    even = [float(weights[HALF]) * s for s in stress]
+    spent = [float(weights[HALF]) * s for s in spent]
+    uneven = [None] * 6
+    for a in range(HALF):
+        here, here_spent = products(a)
+        there, there_spent = products(P_SIZE - 1 - a)
+        weight, moment = float(weights[a]), float(weights[a] * points[a])
+        for k in range(6):
+            even[k] = even[k] + weight * (here[k] + there[k])
+            part = moment * (here[k] - there[k])
+            uneven[k] = part if a == 0 else uneven[k] + part
+        for k in range(3):
+            spent[k] = spent[k] + weight * (here_spent[k] + there_spent[k])
+    return (even, uneven, spent)
+
+
+def element_terms(far, near, spacing, live, contract, weigh):
     slots = spacing.shape[1]
-
-    def grad(field, i, j):
-        column = (3 * field + i) * slots
-        return near[j - 1][:, column : column + slots] if j else far[3 * field + i]
-
-    def product(c, j):
-        return sum(grad(0, i, c) * grad(1, i, j) for i in range(3))
-
-    pairs = [(0, 1), (0, 2), (1, 2)]
-    stack = [product(m, m) for m in range(3)]
-    stack += [product(c, j) + product(j, c) for c, j in pairs]
-    stack += [sum(grad(0, i, j) * grad(0, i, j) for i in range(3)) for j in range(3)]
-    stack_high, stack_low = split(jnp.concatenate(stack, axis=1))
-    both = jnp.dot(contract, stack_high, preferred_element_type=F32)
-    sums = both[:32] + both[32:] + jnp.dot(contract[:32], stack_low, preferred_element_type=F32)
-
-    def part(j, column):
-        return sums[8 * j : 8 * j + 8, column * slots : (column + 1) * slots]
-
     factor = [2.0 / spacing[j : j + 1] for j in range(3)]
     square = [f * f for f in factor]
     jacobian = spacing[0:1] * spacing[1:2] * spacing[2:3] * 0.125
+    rows = [reduced(far, near, r, slots) for r in range(CHUNKS)]
+    lost = 0.0
+    for r in range(CHUNKS):
+        level = sum(square[j] * rows[r][2][j] for j in range(3))
+        lost = lost + weigh[8 * r : 8 * r + 8, :slots] * level
+    blank = jnp.zeros((DEEP - SLAB, slots), F32)
+    columns = [
+        jnp.concatenate([stacked([*[row[p][k] for row in rows], blank]) for p in range(2)], axis=0)
+        for k in range(6)
+    ]
+    sums = jnp.dot(contract, jnp.concatenate(columns, axis=1), preferred_element_type=F32)
+
+    def part(j, column):
+        return sums[8 * j : 8 * j + 8, column * slots : (column + 1) * slots]
+
     terms = []
     for c in range(3):
         total = sum(square[m] * part(c, m) for m in range(3)) - 2.0 * square[c] * part(c, c)
-        for column, pair in enumerate(pairs):
+        for column, pair in enumerate(PAIRS):
             if c in pair:
                 j = pair[0] + pair[1] - c
                 total = total - square[j] * part(j, 3 + column)
         terms.append(jnp.where(live, total * (factor[c] * jacobian), 0.0))
-    spent = sum(square[j] * part(3, 6 + j) for j in range(3)) * jacobian
-    return (terms, jnp.where(live, spent, 0.0))
+    return (terms, jnp.where(live, lost * jacobian, 0.0))
+
+
+def spread(row):
+    return jnp.broadcast_to(row, (16, row.shape[1])).astype(BF16)
 
 
 def place(index, rows, values=None):
     slots = index.shape[1]
-    row = lax.broadcasted_iota(jnp.int32, (rows, slots), 0)
+    row = lax.broadcasted_iota(jnp.int32, (rows, slots), 0).astype(F32).astype(BF16)
+    index = index.astype(F32)
+    zero = jnp.zeros((rows, slots), BF16)
     columns = []
     for k in range(8):
-        hit = row == index[k : k + 1]
+        hit = row == jnp.concatenate([spread(index[k : k + 1])] * (rows // 16), axis=0)
         if values is None:
-            columns.append(jnp.where(hit, 1.0, 0.0).astype(BF16))
+            columns.append(jnp.where(hit, jnp.ones_like(zero), zero))
         else:
             columns.append(
-                jnp.concatenate(
-                    [jnp.where(hit, v[k : k + 1], 0.0).astype(BF16) for v in values], axis=0
-                )
+                jnp.concatenate([jnp.where(hit, spread(v[k : k + 1]), zero) for v in values], axis=0)
             )
     return jnp.concatenate(columns, axis=1)
 
@@ -190,10 +262,10 @@
 
 def kernel(
     groups, columns,
-    velocity_in, adjoint_in, spacing_in, count_in, map_in, head_in, tail_in, contract_in,
+    velocity_in, adjoint_in, spacing_in, count_in, map_in, table_in, contract_in, weigh_in,
     direction, objective,
-    velocity, adjoint, spacing, count, design_map, head, tail, contract, far,
-    outgoing, arrived, gathered,
+    velocity, adjoint, spacing, count, design_map, table, contract, weigh, near, far,
+    outgoing, arrived, gathered_sums, gathered,
     local_sem, send_sem, recv_sem, hand_sem, send_all, recv_all,
 ):
     devices = groups * columns
@@ -203,8 +275,9 @@
 
     barrier = pltpu.get_barrier_semaphore()
     pairs = [
-        (velocity_in, velocity), (adjoint_in, adjoint), (head_in, head), (tail_in, tail),
-        (map_in, design_map), (spacing_in, spacing), (count_in, count), (contract_in, contract),
+        (velocity_in, velocity), (adjoint_in, adjoint), (table_in, table),
+        (map_in, design_map), (spacing_in, spacing), (count_in, count),
+        (contract_in, contract), (weigh_in, weigh),
     ]
     loads = [pltpu.make_async_copy(a, b, local_sem.at[i]) for i, (a, b) in enumerate(pairs)]
     for load in loads:
@@ -219,14 +292,13 @@
     everyone += [(0, turn) for turn in range(1, columns)]
     for step, turn in everyone:
         pl.semaphore_signal(barrier, inc=1, device_id=at(step, turn), device_id_type=MESH)
-    for load in loads[:4]:
+    for load in loads[:3]:
         load.wait()
 
-    fields = jnp.concatenate([f[i] for f in (velocity, adjoint) for i in range(3)], axis=1)
-    near = near_derivatives(fields, head, tail)
+    near_derivatives(velocity, adjoint, table, near)
     far_derivatives(velocity, adjoint, far)
 
-    for load in loads[4:]:
+    for load in loads[3:]:
         load.wait()
     odd = lax.rem(col, 2)
     partner = col + 1 - 2 * odd
@@ -267,15 +339,15 @@
         return groups + parity * (groups - 1) + step
 
     messages = []
+    messages.append(message(0, (grp, partner)))
+    messages.append(message(1, (grp, outer)))
     for step in steps:
-        there = lax.rem(grp + step, groups)
-        messages.append(message(along(odd, step), (there, col + 1 - odd)))
-        messages.append(message(1 + step, (there, outer)))
-    messages.append(message(1, (grp, outer)))
-    messages.append(message(0, (grp, partner)))
+        messages.append(message(along(odd, step), (lax.rem(grp + step, groups), col + 1 - odd)))
+    for step in steps:
+        messages.append(message(1 + step, (lax.rem(grp + step, groups), outer)))
 
     live = lax.broadcasted_iota(jnp.int32, (8, slots), 1) < count[0]
-    terms, spent = element_terms(far, near, spacing[...], live, contract[...])
+    terms, spent = element_terms(far, near, spacing[...], live, contract[...], weigh[...])
     for c in range(3):
         outgoing[8 * c : 8 * c + 8, :] = terms[c]
     outgoing[24:32, :] = design_map[...].astype(F32)
@@ -285,33 +357,57 @@
 
     base = me * UPPER
 
-    def collect(block):
-        nodes = block[24:32].astype(jnp.int32)
-        term = block[:24]
-        lower = place(nodes & (LANES - 1), LANES)
-        index = lax.shift_right_logical(nodes, jnp.full_like(nodes, LANES.bit_length() - 1)) - base
-        highs = [term[8 * c : 8 * c + 8].astype(BF16).astype(F32) for c in range(3)]
-        lows = [term[8 * c : 8 * c + 8] - highs[c] for c in range(3)]
+    def collect(blocks):
+        uppers, lowers = [], []
+        for block in blocks:
+            nodes, term = block[24:32].astype(jnp.int32), block[:24]
+            index = lax.shift_right_logical(nodes, jnp.full_like(nodes, LANES.bit_length() - 1)) - base
+            highs = [term[8 * c : 8 * c + 8].astype(BF16).astype(F32) for c in range(3)]
+            lows = [term[8 * c : 8 * c + 8] - highs[c] for c in range(3)]
+            uppers.append(place(index, UPPER, highs + lows))
+            lowers.append(place(nodes & (LANES - 1), LANES))
         return lax.dot_general(
-            place(index, UPPER, highs + lows),
-            lower,
+            jnp.concatenate(uppers, axis=1),
+            jnp.concatenate(lowers, axis=1),
             (((1,), (1,)), ((), ())),
             preferred_element_type=F32,
         )
 
-    both = collect(outgoing[...])
-    order = [(0, False), (1, False)]
-    for step in steps[::-1]:
-        order += [(along(0, step), True), (along(1, step), True), (1 + step, False)]
-    for slot, shared in order:
+    def arrive(slot):
         hand_on(slot).wait_recv()
-        if shared:
-
-            @pl.when(odd == 1)
-            def _():
-                hand_on(slot).start()
-
-        both = both + collect(arrived[slot])
+
+    near_first = steps[::-1]
+    shared = [along(parity, step) for step in near_first for parity in range(2)]
+    direct = [1 + step for step in [0, *near_first]]
+
+    def add(slots_in):
+        gathered_sums[...] += collect([arrived[slot] for slot in slots_in])
+
+    both = collect([outgoing[...]])
+    arrive(0)
+    gathered_sums[...] = both + collect([arrived[0]])
+
+    @pl.when(odd == 1)
+    def _():
+        for slot in shared:
+            arrive(slot)
+            hand_on(slot).start()
+        arrive(direct[0])
+        add([direct[0], *shared])
+        for slot in direct[1:]:
+            arrive(slot)
+        add(direct[1:])
+
+    @pl.when(odd == 0)
+    def _():
+        for slot in direct:
+            arrive(slot)
+        add(direct)
+        for slot in shared:
+            arrive(slot)
+        add(shared)
+
+    both = gathered_sums[...]
     total = both[: 3 * UPPER] + both[3 * UPPER :]
 
     squares = total * total
@@ -391,10 +487,12 @@
             pltpu.VMEM(spacing.shape, F32),
             pltpu.SMEM((1,), jnp.int32),
             pltpu.VMEM((8, slots), jnp.int32),
-            *[pltpu.VMEM(table.shape, BF16) for table in constants],
-            pltpu.VMEM((6, ROWS, slots), F32),
+            *[pltpu.VMEM(table.shape, table.dtype) for table in constants],
+            pltpu.VMEM((P_SIZE, 2 * SLAB, 6 * slots), F32),
+            pltpu.VMEM((6, P_SIZE, SLAB, slots), F32),
             pltpu.VMEM((32, slots), F32),
             pltpu.VMEM((blocks - 1, 32, slots), F32),
+            pltpu.VMEM((6 * UPPER, LANES), F32),
             pltpu.VMEM((devices, 1, LANES), F32),
             pltpu.SemaphoreType.DMA((8,)),
             pltpu.SemaphoreType.DMA,

time: 20.7 us -> 19.1 us (0.923)
  Pallas kernels: 19.3 us -> 17.7 us
    pallas_call x1, Pallas kernels: 18.7 us -> 17.1 us  [body(): pl.pallas_call(functools.partial(kernel, groups, columns), out_shape=(jax...]
where the time goes in v3:
time: 19.1 us; the launch traced here: 19 us
  Pallas kernels  17.7 us (93%)
  between operations  1.28 us (7%)
    pallas_call x1, Pallas kernels, body(): pl.pallas_call(functools.partial(kernel, groups, columns), out_shape=(jax...  17.1 us
    pallas_call x1, Pallas kernels, body(): pl.pallas_call(hand_over, out_shape=(jax.ShapeDtypeStruct((3, ND_DEV), F3...  0.64 us

profile of v3, /device:TPU:0, one launch (start us, length us, event | category | flops | bytes accessed | tf_op | source)
XLA Modules:
  0.0 19.0 jit_solution(15342948733539209583)
XLA Ops:
  1.3 17.1 %shard_map.95 = (f32[3,16,128]{2,1,0:T(8,128)S(1)}, f32[1,128]{1,0:T(1,128)S(1)}) custom-call(f32[3,343,128]{2,1,0:T(8,128)} %velocity_in.1, f32[3,343,128]{2,1,0:T(8,128)} %adjoint_in.1, f32[3,128]{1,0:T(4,128)} %spacing_in.1, s32[1]{0:T(128)S(6)} %copy.10.count_in, s32[8,128]{1,0:T(8,128)} %map_in.1, bf16[112,192]{1,0:T(8,128)(2,1)} %constant.6.clone.table_in, ...), custom_call_target="tpu_custom_call" | custom-call | tf_op jit(solution)/shard_map/pallas_call | solution.py:476
  18.3 0.6 %shard_map.96 = (f32[3,2048]{1,0:T(4,128)}, f32[1,1]{1,0:T(1,128)}) custom-call(f32[3,16,128]{2,1,0:T(8,128)S(1)} %get-tuple-element.6.scaled, f32[1,128]{1,0:T(1,128)S(1)} %get-tuple-element.7.spent), custom_call_target="tpu_custom_call" | custom-call | tf_op jit(solution)/shard_map/pallas_call | solution.py:506

commit v4 on v3

--- a/solution.py
+++ b/solution.py
@@ -89,13 +89,17 @@
         even[16 + vertex] = signs[2] / 4.0 * first * face
         uneven[8 + vertex] = signs[0] * even[8 + vertex]
         uneven[16 + vertex] = signs[0] * even[16 + vertex]
-    weigh = np.zeros((SLAB, LANES), np.float32)
-    weigh[:FACE] = face[:, None]
-    return (
-        np.concatenate(near, axis=0),
-        np.concatenate([triple(even, 32), triple(uneven, 32)], axis=1),
-        weigh,
-    )
+    return np.concatenate([*near, triple(even, 32), triple(uneven, 32)], axis=0)
+
+
+def face_weights(r, slots):
+    points, weights = quadrature()
+    face = np.outer(weights, weights).reshape(-1)
+    row = lax.broadcasted_iota(jnp.int32, (8, slots), 0)
+    value = jnp.zeros((8, slots), F32)
+    for k, weight in enumerate(face[8 * r : 8 * r + 8]):
+        value = jnp.where(row == k, float(weight), value)
+    return value
 
 
 def split(value):
@@ -129,7 +133,7 @@
             for i in range(3)
         ]
         near[a] = jnp.dot(
-            table[...], jnp.concatenate(fields, axis=1), preferred_element_type=F32
+            table[: 2 * SLAB], jnp.concatenate(fields, axis=1), preferred_element_type=F32
         )
 
 
@@ -195,7 +199,7 @@
     return (even, uneven, spent)
 
 
-def element_terms(far, near, spacing, live, contract, weigh):
+def element_terms(far, near, spacing, live, table):
     slots = spacing.shape[1]
     factor = [2.0 / spacing[j : j + 1] for j in range(3)]
     square = [f * f for f in factor]
@@ -204,13 +208,17 @@
     lost = 0.0
     for r in range(CHUNKS):
         level = sum(square[j] * rows[r][2][j] for j in range(3))
-        lost = lost + weigh[8 * r : 8 * r + 8, :slots] * level
+        lost = lost + face_weights(r, slots) * level
     blank = jnp.zeros((DEEP - SLAB, slots), F32)
-    columns = [
-        jnp.concatenate([stacked([*[row[p][k] for row in rows], blank]) for p in range(2)], axis=0)
-        for k in range(6)
-    ]
-    sums = jnp.dot(contract, jnp.concatenate(columns, axis=1), preferred_element_type=F32)
+    sums = 0.0
+    for p in range(2):
+        columns = [stacked([*[row[p][k] for row in rows], blank]) for k in range(6)]
+        begin = 2 * SLAB + 32 * p
+        sums = sums + jnp.dot(
+            table[begin : begin + 32],
+            jnp.concatenate(columns, axis=1),
+            preferred_element_type=F32,
+        )
 
     def part(j, column):
         return sums[8 * j : 8 * j + 8, column * slots : (column + 1) * slots]
@@ -262,9 +270,9 @@
 
 def kernel(
     groups, columns,
-    velocity_in, adjoint_in, spacing_in, count_in, map_in, table_in, contract_in, weigh_in,
+    velocity_in, adjoint_in, spacing_in, count_in, map_in, table_in,
     direction, objective,
-    velocity, adjoint, spacing, count, design_map, table, contract, weigh, near, far,
+    velocity, adjoint, spacing, count, design_map, table, near, far,
     outgoing, arrived, gathered_sums, gathered,
     local_sem, send_sem, recv_sem, hand_sem, send_all, recv_all,
 ):
@@ -277,7 +285,6 @@
     pairs = [
         (velocity_in, velocity), (adjoint_in, adjoint), (table_in, table),
         (map_in, design_map), (spacing_in, spacing), (count_in, count),
-        (contract_in, contract), (weigh_in, weigh),
     ]
     loads = [pltpu.make_async_copy(a, b, local_sem.at[i]) for i, (a, b) in enumerate(pairs)]
     for load in loads:
@@ -304,25 +311,29 @@
     partner = col + 1 - 2 * odd
     outer = lax.rem(col + 2 * odd + columns - 1, columns)
 
-    def message(slot, there):
+    def message(slot, there, wait):
         return pltpu.make_async_remote_copy(
             src_ref=outgoing,
             dst_ref=arrived.at[slot],
             send_sem=send_sem,
-            recv_sem=recv_sem.at[slot],
+            recv_sem=recv_sem.at[wait],
             device_id=there,
             device_id_type=MESH,
         )
 
-    def hand_on(slot):
+    def arriving(slot, count, wait):
+        part = arrived.at[pl.ds(slot, count)]
         return pltpu.make_async_remote_copy(
-            src_ref=arrived.at[slot],
-            dst_ref=arrived.at[slot],
+            src_ref=part,
+            dst_ref=part,
             send_sem=hand_sem,
-            recv_sem=recv_sem.at[slot],
+            recv_sem=recv_sem.at[wait],
             device_id=(grp, partner),
             device_id_type=MESH,
         )
+
+    def pair(step):
+        return arriving(along(0, step), 2, 2 + step)
 
     def whole(ref, count, semaphore):
         part = ref.at[pl.ds(0, count)]
@@ -336,18 +347,18 @@
         )
 
     def along(parity, step):
-        return groups + parity * (groups - 1) + step
+        return groups + 2 * step - 1 + parity
 
     messages = []
-    messages.append(message(0, (grp, partner)))
-    messages.append(message(1, (grp, outer)))
+    messages.append(message(0, (grp, partner), 0))
+    messages.append(message(1, (grp, outer), 1))
     for step in steps:
-        messages.append(message(along(odd, step), (lax.rem(grp + step, groups), col + 1 - odd)))
-    for step in steps:
-        messages.append(message(1 + step, (lax.rem(grp + step, groups), outer)))
+        there = lax.rem(grp + step, groups)
+        messages.append(message(along(odd, step), (there, col + 1 - odd), 2 + step))
+        messages.append(message(1 + step, (there, outer), 2))
 
     live = lax.broadcasted_iota(jnp.int32, (8, slots), 1) < count[0]
-    terms, spent = element_terms(far, near, spacing[...], live, contract[...], weigh[...])
+    terms, spent = element_terms(far, near, spacing[...], live, table)
     for c in range(3):
         outgoing[8 * c : 8 * c + 8, :] = terms[c]
     outgoing[24:32, :] = design_map[...].astype(F32)
@@ -373,38 +384,35 @@
             preferred_element_type=F32,
         )
 
-    def arrive(slot):
-        hand_on(slot).wait_recv()
-
     near_first = steps[::-1]
     shared = [along(parity, step) for step in near_first for parity in range(2)]
-    direct = [1 + step for step in [0, *near_first]]
+    direct = [1 + step for step in range(1, groups)]
 
     def add(slots_in):
         gathered_sums[...] += collect([arrived[slot] for slot in slots_in])
 
     both = collect([outgoing[...]])
-    arrive(0)
+    arriving(0, 1, 0).wait_recv()
     gathered_sums[...] = both + collect([arrived[0]])
 
     @pl.when(odd == 1)
     def _():
-        for slot in shared:
-            arrive(slot)
-            hand_on(slot).start()
-        arrive(direct[0])
-        add([direct[0], *shared])
-        for slot in direct[1:]:
-            arrive(slot)
-        add(direct[1:])
+        for step in near_first:
+            pair(step).wait_recv()
+            pair(step).start()
+        arriving(1, 1, 1).wait_recv()
+        add([1, *shared])
+        arriving(2, groups - 1, 2).wait_recv()
+        add(direct)
 
     @pl.when(odd == 0)
     def _():
-        for slot in direct:
-            arrive(slot)
+        arriving(1, 1, 1).wait_recv()
+        add([1])
+        arriving(2, groups - 1, 2).wait_recv()
         add(direct)
-        for slot in shared:
-            arrive(slot)
+        for step in near_first:
+            pair(step).wait_recv()
         add(shared)
 
     both = gathered_sums[...]
@@ -463,7 +471,7 @@
     blocks = 3 * groups
     slots = spacing.shape[1]
     vmem = pl.BlockSpec(memory_space=pltpu.VMEM)
-    constants = tables()
+    constant = tables()
     operands = [
         pltpu.with_memory_space_constraint(jnp.asarray(x), pltpu.HBM)
         for x in (velocity, adjoint, spacing)
@@ -471,7 +479,7 @@
     operands.append(elem_count)
     operands += [
         pltpu.with_memory_space_constraint(jnp.asarray(x), pltpu.HBM)
-        for x in (design_map, *constants)
+        for x in (design_map, constant)
     ]
     scaled, spent = pl.pallas_call(
         functools.partial(kernel, groups, columns),
@@ -479,7 +487,7 @@
             jax.ShapeDtypeStruct((3, UPPER, LANES), F32),
             jax.ShapeDtypeStruct((1, LANES), F32),
         ),
-        in_specs=[pl.BlockSpec(memory_space=pltpu.HBM)] * 8,
+        in_specs=[pl.BlockSpec(memory_space=pltpu.HBM)] * 6,
         out_specs=(vmem, vmem),
         scratch_shapes=[
             pltpu.VMEM(velocity.shape, F32),
@@ -487,16 +495,16 @@
             pltpu.VMEM(spacing.shape, F32),
             pltpu.SMEM((1,), jnp.int32),
             pltpu.VMEM((8, slots), jnp.int32),
-            *[pltpu.VMEM(table.shape, table.dtype) for table in constants],
+            pltpu.VMEM(constant.shape, BF16),
             pltpu.VMEM((P_SIZE, 2 * SLAB, 6 * slots), F32),
             pltpu.VMEM((6, P_SIZE, SLAB, slots), F32),
             pltpu.VMEM((32, slots), F32),
             pltpu.VMEM((blocks - 1, 32, slots), F32),
             pltpu.VMEM((6 * UPPER, LANES), F32),
             pltpu.VMEM((devices, 1, LANES), F32),
-            pltpu.SemaphoreType.DMA((8,)),
+            pltpu.SemaphoreType.DMA((6,)),
             pltpu.SemaphoreType.DMA,
-            pltpu.SemaphoreType.DMA((blocks - 1,)),
+            pltpu.SemaphoreType.DMA((groups + 2,)),
             *[pltpu.SemaphoreType.DMA] * 3,
         ],
         compiler_params=pltpu.CompilerParams(

time: 19.1 us -> 18.6 us (0.974)
  Pallas kernels: 17.7 us -> 17.2 us
    pallas_call x1, Pallas kernels: 17.1 us -> 16.5 us  [body(): pl.pallas_call(functools.partial(kernel, groups, columns), out_shape=(jax...]
where the time goes in v4:
time: 18.6 us; the launch traced here: 18.5 us
  Pallas kernels  17.2 us (92%)
  between operations  1.28 us (7%)
    pallas_call x1, Pallas kernels, body(): pl.pallas_call(functools.partial(kernel, groups, columns), out_shape=(jax...  16.5 us
    pallas_call x1, Pallas kernels, body(): pl.pallas_call(hand_over, out_shape=(jax.ShapeDtypeStruct((3, ND_DEV), F3...  0.64 us

profile of v4, /device:TPU:0, one launch (start us, length us, event | category | flops | bytes accessed | tf_op | source)
XLA Modules:
  0.0 18.5 jit_solution(7168327777171252204)
XLA Ops:
  1.3 16.5 %shard_map.77 = (f32[3,16,128]{2,1,0:T(8,128)S(1)}, f32[1,128]{1,0:T(1,128)S(1)}) custom-call(f32[3,343,128]{2,1,0:T(8,128)} %velocity_in.1, f32[3,343,128]{2,1,0:T(8,128)} %adjoint_in.1, f32[3,128]{1,0:T(4,128)} %spacing_in.1, s32[1]{0:T(128)S(6)} %copy.8.count_in, s32[8,128]{1,0:T(8,128)} %map_in.1, bf16[176,192]{1,0:T(8,128)(2,1)} %constant.2.clone.table_in), custom_call_target="tpu_custom_call" | custom-call | tf_op jit(solution)/shard_map/pallas_call | solution.py:484
  17.8 0.6 %shard_map.78 = (f32[3,2048]{1,0:T(4,128)}, f32[1,1]{1,0:T(1,128)}) custom-call(f32[3,16,128]{2,1,0:T(8,128)S(1)} %get-tuple-element.6.scaled, f32[1,128]{1,0:T(1,128)S(1)} %get-tuple-element.7.spent), custom_call_target="tpu_custom_call" | custom-call | tf_op jit(solution)/shard_map/pallas_call | solution.py:514

commit v5 on v4

--- a/solution.py
+++ b/solution.py
@@ -313,7 +313,7 @@
 
     def message(slot, there, wait):
         return pltpu.make_async_remote_copy(
-            src_ref=outgoing,
+            src_ref=outgoing.at[0],
             dst_ref=arrived.at[slot],
             send_sem=send_sem,
             recv_sem=recv_sem.at[wait],
@@ -360,8 +360,8 @@
     live = lax.broadcasted_iota(jnp.int32, (8, slots), 1) < count[0]
     terms, spent = element_terms(far, near, spacing[...], live, table)
     for c in range(3):
-        outgoing[8 * c : 8 * c + 8, :] = terms[c]
-    outgoing[24:32, :] = design_map[...].astype(F32)
+        outgoing[0, 7 * c : 7 * c + 7, :] = terms[c][:7]
+    outgoing[0, 21:29, :] = design_map[...].astype(F32)
     pl.semaphore_wait(barrier, devices - 1)
     for copy in messages:
         copy.start()
@@ -370,11 +370,15 @@
 
     def collect(blocks):
         uppers, lowers = [], []
-        for block in blocks:
-            nodes, term = block[24:32].astype(jnp.int32), block[:24]
+        for ref, slot in blocks:
+            nodes = ref[slot, 21:29, :].astype(jnp.int32)
             index = lax.shift_right_logical(nodes, jnp.full_like(nodes, LANES.bit_length() - 1)) - base
-            highs = [term[8 * c : 8 * c + 8].astype(BF16).astype(F32) for c in range(3)]
-            lows = [term[8 * c : 8 * c + 8] - highs[c] for c in range(3)]
+            highs, lows = [], []
+            for c in range(3):
+                term = ref[slot, 7 * c : 7 * c + 7, :]
+                term = jnp.concatenate([term, -jnp.sum(term, axis=0, keepdims=True)], axis=0)
+                highs.append(term.astype(BF16).astype(F32))
+                lows.append(term - highs[c])
             uppers.append(place(index, UPPER, highs + lows))
             lowers.append(place(nodes & (LANES - 1), LANES))
         return lax.dot_general(
@@ -384,20 +388,22 @@
             preferred_element_type=F32,
         )
 
-    near_first = steps[::-1]
-    shared = [along(parity, step) for step in near_first for parity in range(2)]
+    edge = lax.rem(grp, groups - 1) == 0
+    expected = [jnp.where(edge, a, b) for a, b in zip(steps, steps[::-1])]
+    shared = [along(parity, step) for step in expected for parity in range(2)]
     direct = [1 + step for step in range(1, groups)]
 
     def add(slots_in):
-        gathered_sums[...] += collect([arrived[slot] for slot in slots_in])
-
-    both = collect([outgoing[...]])
+        gathered_sums[...] += collect([(arrived, slot) for slot in slots_in])
+
+    gathered[devices - 1, 1:2] = jnp.sum(spent, axis=0, keepdims=True)
+    both = collect([(outgoing, 0)])
     arriving(0, 1, 0).wait_recv()
-    gathered_sums[...] = both + collect([arrived[0]])
+    gathered_sums[...] = both + collect([(arrived, 0)])
 
     @pl.when(odd == 1)
     def _():
-        for step in near_first:
+        for step in expected:
             pair(step).wait_recv()
             pair(step).start()
         arriving(1, 1, 1).wait_recv()
@@ -411,22 +417,18 @@
         add([1])
         arriving(2, groups - 1, 2).wait_recv()
         add(direct)
-        for step in near_first:
+        for step in expected[:-1]:
             pair(step).wait_recv()
-        add(shared)
+        add(shared[:-2])
+        pair(expected[-1]).wait_recv()
+        add(shared[-2:])
 
     both = gathered_sums[...]
     total = both[: 3 * UPPER] + both[3 * UPPER :]
 
     squares = total * total
     squares = sum(squares[8 * i : 8 * i + 8] for i in range(3 * UPPER // 8))
-    lane = lax.broadcasted_iota(jnp.int32, (8, LANES), 1)
-    mixed = jnp.where(
-        lane < LANES // 2,
-        squares + pltpu.roll(squares, LANES // 2, 1),
-        spent + pltpu.roll(spent, LANES // 2, 1),
-    )
-    gathered[devices - 1] = jnp.sum(mixed, axis=0, keepdims=True)
+    gathered[devices - 1, 0:1] = jnp.sum(squares, axis=0, keepdims=True)
 
     def share(step, turn):
         slot = step * columns + turn - 1
@@ -444,9 +446,8 @@
     whole(arrived, len(messages), send_sem).wait_send()
     whole(gathered, devices - 1, recv_all).wait_recv()
     everything = jnp.sum(gathered[...], axis=0)
-    first = lax.broadcasted_iota(jnp.int32, (1, LANES), 1) < LANES // 2
-    square_total = jnp.sum(jnp.where(first, everything, 0.0), axis=1, keepdims=True)
-    spent_total = jnp.sum(jnp.where(first, 0.0, everything), axis=1, keepdims=True)
+    totals = jnp.sum(everything, axis=1, keepdims=True)
+    square_total, spent_total = totals[:1], totals[1:]
     scale = lax.rsqrt(square_total * (1.0 / (3.0 * ND_DEV * devices)) + 1e-06)
     scaled = total * scale
     for c in range(3):
@@ -498,10 +499,10 @@
             pltpu.VMEM(constant.shape, BF16),
             pltpu.VMEM((P_SIZE, 2 * SLAB, 6 * slots), F32),
             pltpu.VMEM((6, P_SIZE, SLAB, slots), F32),
-            pltpu.VMEM((32, slots), F32),
-            pltpu.VMEM((blocks - 1, 32, slots), F32),
+            pltpu.VMEM((1, 29, slots), F32),
+            pltpu.VMEM((blocks - 1, 29, slots), F32),
             pltpu.VMEM((6 * UPPER, LANES), F32),
-            pltpu.VMEM((devices, 1, LANES), F32),
+            pltpu.VMEM((devices, 2, LANES), F32),
             pltpu.SemaphoreType.DMA((6,)),
             pltpu.SemaphoreType.DMA,
             pltpu.SemaphoreType.DMA((groups + 2,)),

time: 18.6 us -> 18.5 us (level)
  Pallas kernels: 17.2 us -> 17 us
where the time goes in v5:
time: 18.5 us; the launch traced here: 18.3 us
  Pallas kernels  17 us (92%)
  between operations  1.28 us (7%)
    pallas_call x1, Pallas kernels, body(): pl.pallas_call(functools.partial(kernel, groups, columns), out_shape=(jax...  16.4 us
    pallas_call x1, Pallas kernels, body(): pl.pallas_call(hand_over, out_shape=(jax.ShapeDtypeStruct((3, ND_DEV), F3...  0.64 us

profile of v5, /device:TPU:0, one launch (start us, length us, event | category | flops | bytes accessed | tf_op | source)
XLA Modules:
  0.0 18.3 jit_solution(2169986782878336164)
XLA Ops:
  1.3 16.4 %shard_map.77 = (f32[3,16,128]{2,1,0:T(8,128)S(1)}, f32[1,128]{1,0:T(1,128)S(1)}) custom-call(f32[3,343,128]{2,1,0:T(8,128)} %velocity_in.1, f32[3,343,128]{2,1,0:T(8,128)} %adjoint_in.1, f32[3,128]{1,0:T(4,128)} %spacing_in.1, s32[1]{0:T(128)S(6)} %copy.8.count_in, s32[8,128]{1,0:T(8,128)} %map_in.1, bf16[176,192]{1,0:T(8,128)(2,1)} %constant.2.clone.table_in), custom_call_target="tpu_custom_call" | custom-call | tf_op jit(solution)/shard_map/pallas_call | solution.py:485
  17.7 0.6 %shard_map.78 = (f32[3,2048]{1,0:T(4,128)}, f32[1,1]{1,0:T(1,128)}) custom-call(f32[3,16,128]{2,1,0:T(8,128)S(1)} %get-tuple-element.6.scaled, f32[1,128]{1,0:T(1,128)S(1)} %get-tuple-element.7.spent), custom_call_target="tpu_custom_call" | custom-call | tf_op jit(solution)/shard_map/pallas_call | solution.py:515

commit v6 on v5

--- a/solution.py
+++ b/solution.py
@@ -286,18 +286,20 @@
         (velocity_in, velocity), (adjoint_in, adjoint), (table_in, table),
         (map_in, design_map), (spacing_in, spacing), (count_in, count),
     ]
+    steps = far_first(groups, grp)
+
+    def at(step, turn):
+        return (lax.rem(grp + step, groups), lax.rem(col + turn, columns))
+
+    everyone = [(step, turn) for step in steps for turn in range(columns)]
+    everyone += [(0, turn) for turn in range(1, columns)]
+    for step, turn in everyone[:columns]:
+        pl.semaphore_signal(barrier, inc=1, device_id=at(step, turn), device_id_type=MESH)
     loads = [pltpu.make_async_copy(a, b, local_sem.at[i]) for i, (a, b) in enumerate(pairs)]
     for load in loads:
         load.start()
 
-    steps = far_first(groups, grp)
-
-    def at(step, turn):
-        return (lax.rem(grp + step, groups), lax.rem(col + turn, columns))
-
-    everyone = [(step, turn) for step in steps for turn in range(columns)]
-    everyone += [(0, turn) for turn in range(1, columns)]
-    for step, turn in everyone:
+    for step, turn in everyone[columns:]:
         pl.semaphore_signal(barrier, inc=1, device_id=at(step, turn), device_id_type=MESH)
     for load in loads[:3]:
         load.wait()
@@ -444,6 +446,11 @@
     for step, turn in everyone:
         share(step, turn).start()
     whole(arrived, len(messages), send_sem).wait_send()
+    @pl.when(odd == 1)
+    def _():
+        whole(arrived, 2 * (groups - 1), hand_sem).wait_send()
+
+    whole(gathered, devices - 1, send_all).wait_send()
     whole(gathered, devices - 1, recv_all).wait_recv()
     everything = jnp.sum(gathered[...], axis=0)
     totals = jnp.sum(everything, axis=1, keepdims=True)
@@ -453,11 +460,6 @@
     for c in range(3):
         direction[c] = scaled[UPPER * c : UPPER * c + UPPER]
     objective[...] = jnp.broadcast_to(spent_total * (1.0 / (NODES * slots * devices)), (1, LANES))
-    whole(gathered, devices - 1, send_all).wait_send()
-
-    @pl.when(odd == 1)
-    def _():
-        whole(arrived, 2 * (groups - 1), hand_sem).wait_send()
 
 
 def hand_over(scaled, spent, direction, objective):

time: 18.5 us -> 18.5 us (level)
  no operation moved by 1% of the time
where the time goes in v6:
time: 18.5 us; the launch traced here: 18.3 us
  Pallas kernels  17 us (92%)
  between operations  1.28 us (7%)
    pallas_call x1, Pallas kernels, body(): pl.pallas_call(functools.partial(kernel, groups, columns), out_shape=(jax...  16.4 us
    pallas_call x1, Pallas kernels, body(): pl.pallas_call(hand_over, out_shape=(jax.ShapeDtypeStruct((3, ND_DEV), F3...  0.64 us

profile of v6, /device:TPU:0, one launch (start us, length us, event | category | flops | bytes accessed | tf_op | source)
XLA Modules:
  0.0 18.3 jit_solution(10416154286879634863)
XLA Ops:
  1.3 16.4 %shard_map.77 = (f32[3,16,128]{2,1,0:T(8,128)S(1)}, f32[1,128]{1,0:T(1,128)S(1)}) custom-call(f32[3,343,128]{2,1,0:T(8,128)} %velocity_in.1, f32[3,343,128]{2,1,0:T(8,128)} %adjoint_in.1, f32[3,128]{1,0:T(4,128)} %spacing_in.1, s32[1]{0:T(128)S(6)} %copy.8.count_in, s32[8,128]{1,0:T(8,128)} %map_in.1, bf16[176,192]{1,0:T(8,128)(2,1)} %constant.2.clone.table_in), custom_call_target="tpu_custom_call" | custom-call | tf_op jit(solution)/shard_map/pallas_call | solution.py:487
  17.7 0.6 %shard_map.78 = (f32[3,2048]{1,0:T(4,128)}, f32[1,1]{1,0:T(1,128)}) custom-call(f32[3,16,128]{2,1,0:T(8,128)S(1)} %get-tuple-element.6.scaled, f32[1,128]{1,0:T(1,128)S(1)} %get-tuple-element.7.spent), custom_call_target="tpu_custom_call" | custom-call | tf_op jit(solution)/shard_map/pallas_call | solution.py:517
